TPU v7x, 32 devices: a whole 2x2x4 slice. The times are simulated.
32 devices in a mesh: groups: 2 (over x), tp: 8 (over z, y), blk: 2 (over core).
Axes of the slice: x: 2, y: 2, z: 4, core: 2. Of those that a mesh axis runs over, the one named last changes fastest.
Arguments:
- tokens: bfloat16 [4096, 7168], P(('groups', 'tp')), parts along dimension 0, may hold values from -6 to 6
- gate_weight: bfloat16 [7168, 2048], P('tp', 'blk'), may hold values from -0.0625 to 0.0625
- up_weight: bfloat16 [7168, 2048], P('tp', 'blk'), may hold values from -0.0625 to 0.0625
- down_weight: bfloat16 [2048, 7168], P('blk', 'tp'), may hold values from -0.125 to 0.125
Outputs:
- mixed: bfloat16 [4096, 7168], P(('groups', 'blk'), 'tp'), parts along dimension 0
There are 2 independent parts, one for each index of `groups`. A program takes and returns all parts, laid end to end along the dimension named above; an argument that names none is the same for every part. Nothing has to cross between parts.
All inputs are finite; a program needn't handle non-finite values.
Results may differ from a plain program's by a relative error of at most 0.005.
Values may be sent and summed in bfloat16 or wider, within the bound.
A program may use at most 128 MiB of HBM per device.

v0:
```python
import functools

import jax
import jax.numpy as jnp
from jax import lax
from jax.experimental import pallas as pl
from jax.experimental.pallas import tpu as pltpu
from jax.sharding import PartitionSpec as P

MESH = pl.DeviceIdType.MESH
ANY = pl.BlockSpec(memory_space=pl.ANY)


def flip1(i):
    return i + 1 - 2 * (i % 2)


def greet(devices):
    barrier = pltpu.get_barrier_semaphore()
    for device in devices:
        pl.semaphore_signal(barrier, inc=1, device_id=device, device_id_type=MESH)
    pl.semaphore_wait(barrier, len(devices))


def flip2(i):
    return i + 2 - 4 * ((i // 2) % 2)


CUT = 8


def layer(
    G, n, B,
    tok, gate, up, down, out,
    T, W, D, both, mine_h, H, total,
    lsem, tok_send, tok_recv, core_send, core_recv,
    w_send, w_recv, x_send, x_recv, d_send, d_recv,
    h_send, h_recv, f_send, f_recv,
):
    g, t, b = lax.axis_index("groups"), lax.axis_index("tp"), lax.axis_index("blk")
    h = n // B
    a, j = t // h, t % h
    half, pairs = h // 2, n // 2
    p, y = t // 2, t % 2
    other = (g, t, 1 - b)
    across = (g, flip1(t), b)
    R, K = tok.shape
    width = K // B
    depth, units = gate.shape[0], gate.shape[1] // h
    part = depth // G
    mine = pl.ds(pl.multiple_of(b * width, 128), width)
    theirs = pl.ds(pl.multiple_of((1 - b) * width, 128), width)
    square = h == 4
    cut = R * CUT // 16
    upper, lower_rows = pl.ds(0, cut), pl.ds(cut, R - cut)

    greet(
        [(g, (t + d) % n, b) for d in range(1, n)]
        + [(g, 2 * ((p + d) % pairs) + y, 1 - b) for d in range(1, pairs)]
        + [((g + e) % G, t, b) for e in range(1, G)]
        + [other]
    )

    def remote(src, dst, send, recv, device):
        return pltpu.make_async_remote_copy(
            src_ref=src, dst_ref=dst, send_sem=send, recv_sem=recv,
            device_id=device, device_id_type=MESH,
        )

    pending = []

    def push(*copy):
        c = remote(*copy)
        c.start()
        pending.append(c)

    def local(src, dst, sem):
        return pltpu.make_async_copy(src, dst, sem)

    def rows_of(i, s):
        if square:
            i = flip1(i) if s % 2 else i
            return flip2(i) if s // 2 else i
        return (i + h - s) % h

    def token_block(s):
        return T.at[rows_of(j, s), :, mine]

    def w_block(source, first, size, k):
        start = pl.multiple_of(source * depth + first, 16)
        return W.at[pl.ds(start, size), pl.ds(k * units, units)]

    own_columns = pl.ds(pl.multiple_of(j * units, 128), units)
    loads = [
        local(gate.at[:, own_columns], w_block(t, 0, depth, 0), lsem.at[0]),
        local(up.at[:, own_columns], w_block(t, 0, depth, 1), lsem.at[1]),
        local(tok, T.at[j], lsem.at[2]),
        local(down, D.at[b], lsem.at[3]),
    ]

    first = g * part
    rows = pl.ds(pl.multiple_of(first, 16), part)
    order = [d for k in range(1, n // 2) for d in (k, n - k)] + [n // 2]
    for d in order:
        dest = (t + d) % n
        cols = pl.ds(pl.multiple_of((dest % h) * units, 128), units)
        for k in range(2):
            push(
                (gate, up)[k].at[rows, cols], w_block(t, first, part, k),
                w_send.at[d, k], w_recv.at[d, k], (g, dest, b),
            )

    for s in (2, 1) if square else range(1, h):
        dest = rows_of(j, s) if square else (j + s) % h
        push(tok.at[:, mine], T.at[j, :, mine], tok_send.at[s], tok_recv.at[s], (g, a * h + dest, b))
    push(down, D.at[b], d_send, d_recv, other)
    for load in loads:
        load.start()

    for d in order:
        source = (t + n - d) % n
        for k in range(2):
            block = w_block(source, first, part, k)
            remote(block, block, w_send.at[d, k], w_recv.at[d, k], other).wait_recv()
            for e in range(1, G):
                push(block, block, x_send.at[e, d, k], x_recv.at[e, d, k], ((g + e) % G, t, b))
    for load in loads:
        load.wait()
    remote(D.at[1 - b], D.at[1 - b], d_send, d_recv, other).wait_recv()
    total[...] = jnp.zeros_like(total)

    def tokens_arrive(s):
        block = token_block(s)
        if square and s == 3:
            for i, r in ((3, upper), (0, lower_rows)):
                piece = T.at[rows_of(j, s), r, mine]
                remote(piece, piece, tok_send.at[i], tok_recv.at[i], other).wait_recv()
        else:
            remote(block, block, tok_send.at[s], tok_recv.at[s], other).wait_recv()
        if square and s < 3:
            piece = T.at[rows_of(j, s), (upper, lower_rows)[s - 1], mine]
            target = flip2(j) if s == 1 else flip1(j)
            i = 3 if s == 1 else 0
            push(piece, piece, tok_send.at[i], tok_recv.at[i], (g, a * h + target, b))

        push(block, block, core_send.at[s], core_recv.at[s], other)

    def compute(s):
        slot = rows_of(j, s)
        if s > 0:
            block = T.at[slot, :, theirs]
            remote(block, block, core_send.at[s], core_recv.at[s], other).wait_recv()
        tiles = 4 if K % 512 == 0 else 1
        tile = K // tiles
        both[...] = jnp.zeros_like(both)

        def body(i, carry):
            k = pl.ds(pl.multiple_of(i * tile, 128), tile)
            both[...] += jnp.dot(T[slot, :, k], W[k, :], preferred_element_type=jnp.float32)
            return carry

        lax.fori_loop(0, tiles, body, 0)
        hidden = (jax.nn.silu(both[:, :units]) * both[:, units:]).astype(out.dtype)
        mine_h[s] = hidden

        @pl.when(a == b)
        def _():
            H[s, j, b] = hidden

        for d in sorted(range(1, pairs), key=lambda d: min(d, pairs - d)):
            push(
                mine_h.at[s], H.at[s, j, b], h_send.at[s, d], h_recv.at[s, j // 2, b],
                (g, 2 * ((p + d) % pairs) + y, a),
            )

        @pl.when(a != b)
        def _():
            remote(mine_h.at[s], H.at[s, j, b], h_send.at[s, 0], h_recv.at[s, j // 2, b], other).start()

    def pass_on(s):
        for k in range(half):
            for c in range(B):
                block = H.at[s, 2 * k + y, c]

                @pl.when(jnp.logical_not((a == b) & (j // 2 == k) & (c == b)))
                def _():
                    remote(block, block, h_send.at[s, 0], h_recv.at[s, k, c], other).wait_recv()

                push(block, block, f_send.at[s, k, c], f_recv.at[s, k, c], across)

    def lower(s):
        for k in range(half):
            for c in range(B):
                block = H.at[s, 2 * k + 1 - y, c]
                remote(block, block, f_send.at[s, k, c], f_recv.at[s, k, c], across).wait_recv()

        def body(i, carry):
            r = rows_of(i, s)
            term = total[r]
            for c in range(B):
                term += jnp.dot(
                    H[s, i, c], D[c, pl.ds(pl.multiple_of(i * units, 128), units), :],
                    preferred_element_type=jnp.float32,
                )
            total[r] = term
            return carry

        lax.fori_loop(0, h, body, 0)

    for d in order:
        source = (t + n - d) % n
        for e in range(1, G):
            for k in range(2):
                block = w_block(source, ((g + G - e) % G) * part, part, k)
                remote(block, block, x_send.at[e, d, k], x_recv.at[e, d, k], other).wait_recv()

    compute(0)
    for s in range(1, h):
        tokens_arrive(s)
        compute(s)
        pass_on(s - 1)
        if s >= 2:
            lower(s - 2)
    pass_on(h - 1)
    lower(h - 2)
    lower(h - 1)
    for r in range(h):
        out[pl.ds(r * R, R), :] = total[r].astype(out.dtype)

    for c in pending:
        c.wait_send()
    @pl.when(a != b)
    def _():
        for s in range(h):
            remote(mine_h.at[s], mine_h.at[s], h_send.at[s, 0], h_recv.at[s, 0, 0], other).wait_send()


def local(G, n, B, tokens, gate_weight, up_weight, down_weight):
    h = n // B
    R, K = tokens.shape
    depth, wide = gate_weight.shape
    units, columns = wide // h, down_weight.shape[1]
    dtype = tokens.dtype
    DMA = pltpu.SemaphoreType.DMA
    return pl.pallas_call(
        functools.partial(layer, G, n, B),
        out_shape=jax.ShapeDtypeStruct((h * R, columns), dtype),
        in_specs=[ANY] * 4,
        out_specs=pl.BlockSpec(memory_space=pltpu.VMEM),
        scratch_shapes=[
            pltpu.VMEM((h, R, K), dtype),
            pltpu.VMEM((K, 2 * units), dtype),
            pltpu.VMEM((B, wide, columns), dtype),
            pltpu.VMEM((R, 2 * units), jnp.float32),
            pltpu.VMEM((h, R, units), dtype),
            pltpu.VMEM((h, h, B, R, units), dtype),
            pltpu.VMEM((h, R, columns), jnp.float32),
            DMA((4,)),
            DMA((h,)), DMA((h,)), DMA((h,)), DMA((h,)),
            DMA((n, 2)), DMA((n, 2)),
            DMA((G, n, 2)), DMA((G, n, 2)),
            DMA, DMA,
            DMA((h, n // 2)), DMA((h, h // 2, B)),
            DMA((h, h // 2, B)), DMA((h, h // 2, B)),
        ],
        compiler_params=pltpu.CompilerParams(
            collective_id=0, has_side_effects=True, vmem_limit_bytes=63_000_000
        ),
        name="layer",
    )(tokens, gate_weight, up_weight, down_weight)


def solution(mesh):
    shape = dict(mesh.shape)
    return jax.shard_map(
        functools.partial(local, shape["groups"], shape["tp"], shape["blk"]),
        mesh=mesh,
        in_specs=(P(("groups", "tp"), None), P("tp", "blk"), P("tp", "blk"), P("blk", "tp")),
        out_specs=P(("groups", "blk"), "tp"),
        check_vma=False,
    )
```

profile of v0, /device:TPU:1, one launch (start us, length us, event | category | flops | bytes accessed | tf_op | source)
XLA Modules:
  0.0 184.9 jit_solution(7336265160710775946)
XLA Ops:
  0.0 182.0 %layer.1 = bf16[1024,896]{1,0:T(8,128)(2,1)} custom-call(bf16[256,7168]{1,0:T(8,128)(2,1)} %tok.1, bf16[896,1024]{1,0:T(8,128)(2,1)} %gate.1, bf16[896,1024]{1,0:T(8,128)(2,1)} %up.1, bf16[1024,896]{1,0:T(8,128)(2,1)} %down.1), custom_call_target="tpu_custom_call" | custom-call | tf_op jit(solution)/shard_map/layer/pallas_call | solution.py:245
  182.0 2.9 %copy.6 = bf16[1024,896]{1,0:T(8,128)(2,1)} copy(bf16[1024,896]{1,0:T(8,128)(2,1)} %layer.1) | data formatting | bytes 3670016
where the time goes:
time: 186 us; the launch traced here: 185 us
  Pallas kernels  182 us (98%)
  local copies, waits for them, and re-layouts  2.87 us (2%)
    pallas_call x1, Pallas kernels, local(): pl.pallas_call(functools.partial(layer, G, n, B), out_shape=jax.ShapeDtyp...  182 us

commit v1 on v0

--- a/solution.py
+++ b/solution.py
@@ -270,10 +270,302 @@
     )(tokens, gate_weight, up_weight, down_weight)
 
 
+LANES = 128
+
+
+def column_layer(
+    G, n, B,
+    tok, gate, up, down, out,
+    X, W, D, Q, S, R, S2, R2, hs, H, acc,
+    l_w, l_x, l_d,
+    w_send, w_recv, x_send, x_recv, t_send, t_recv, c_send, c_recv,
+    d_send, d_recv, s_send, s_recv, z_send, z_recv, h_send, h_recv,
+    r_send, r_recv, y_send, y_recv,
+):
+    g, t, b = lax.axis_index("groups"), lax.axis_index("tp"), lax.axis_index("blk")
+    h = n // B
+    z, y, j, a = t // 2, t % 2, t % h, t // h
+    zz = z % 2
+    inner = zz + a == 1
+    outer = zz + a != 1
+    own, foreign = b == a, b != a
+    rows, depth, wide = tok.shape[0], gate.shape[0], gate.shape[1]
+    part = depth // G
+    chunks = wide // LANES
+    mirror = 2 * (n // 2 - 1 - z) + y
+    other = (g, t, 1 - b)
+    beside = (g, flip1(t), b)
+    along = flip2(t)
+    facing = 2 * (n // 2 - 1 - z) + y
+
+    greet(
+        [(g, (t + d) % n, c) for d in range(1, n) for c in range(B)]
+        + [other]
+        + [((g + e) % G, t, b) for e in range(1, G)]
+    )
+
+    def remote(src, dst, send, recv, device):
+        return pltpu.make_async_remote_copy(
+            src_ref=src, dst_ref=dst, send_sem=send, recv_sem=recv,
+            device_id=device, device_id_type=MESH,
+        )
+
+    def push(*copy):
+        remote(*copy).start()
+
+    def got(ref, sem):
+        remote(ref, ref, sem, sem, other).wait_recv()
+
+    def sent(ref, sem):
+        remote(ref, ref, sem, sem, other).wait_send()
+
+    def lanes(k):
+        return pl.ds(pl.multiple_of(k * LANES, LANES), LANES)
+
+    def slice_of(chip):
+        return pl.ds(pl.multiple_of(chip * depth, LANES), depth)
+
+    def mirrored(chip):
+        return 2 * (n // 2 - 1 - chip // 2) + chip % 2
+
+    def partner(d):
+        i = flip1(j) if d % 2 else j
+        return flip2(i) if d // 2 else i
+
+    share = pl.ds(pl.multiple_of(g * part, 16), part)
+    landed = pl.ds(pl.multiple_of(depth + g * part, 16), part)
+
+    def w_piece(c, k):
+        return W.at[c, landed, pl.ds(k * LANES, LANES)]
+
+    def x_block(i, k):
+        return X.at[
+            i % 2, pl.ds(pl.multiple_of(i // 2 * rows, 16), rows),
+            pl.ds(pl.multiple_of(k * depth, LANES), depth),
+        ]
+
+    for c in range(chunks):
+        for k in range(2):
+            push(
+                (gate, up)[k].at[share, lanes(c)], w_piece(c, k),
+                w_send.at[c, k], w_recv.at[c, k], (g, mirror, b),
+            )
+        if c == 0:
+            for d in (3, 1, 2):
+                chip = a * h + partner(d)
+                source = chip + b * (mirrored(chip) - chip)
+                push(tok.at[:, slice_of(source)], x_block(j, b), t_send.at[d], t_recv.at[d], (g, chip, b))
+    loads = []
+    for k, chip in enumerate((t, mirror)):
+        loads.append(pltpu.make_async_copy(tok.at[:, slice_of(chip)], x_block(j, k), l_x.at[k]))
+    for c in range(chunks):
+        for k in range(2):
+            loads.append(pltpu.make_async_copy(
+                (gate, up)[k].at[:, lanes(c)], W.at[c, pl.ds(0, depth), pl.ds(k * LANES, LANES)], l_w.at[c, k],
+            ))
+    for load in loads:
+        load.start()
+    down_loads = []
+
+    def d_block(c, k):
+        return D.at[c, pl.ds(pl.multiple_of(k * LANES, LANES), LANES), :]
+
+    for c in range(chunks):
+        piece = down.at[pl.ds(c * LANES, LANES), :]
+        load = pltpu.make_async_copy(piece, d_block(c, b), l_d.at[c])
+        load.start()
+        down_loads.append(load)
+        push(piece, d_block(c, b), d_send.at[c], d_recv.at[c], other)
+    acc[...] = jnp.zeros_like(acc)
+
+    def weights_arrive(c):
+        for k in range(2):
+            got(w_piece(c, k), w_recv.at[c, k])
+        block = W.at[c, landed, :]
+        for e in range(1, G):
+            push(block, block, x_send.at[e, c], x_recv.at[e, c], ((g + e) % G, t, b))
+
+    def partial_sums(c):
+        for e in range(1, G):
+            start = pl.multiple_of(depth + (g + G - e) % G * part, 16)
+            got(W.at[c, pl.ds(start, part), :], x_recv.at[e, c])
+        S[c] = jnp.dot(X[1 - y], W[c], preferred_element_type=jnp.float32).astype(S.dtype)
+        push(S.at[c], R.at[c], s_send.at[c], s_recv.at[c], beside)
+        Q[c] = jnp.dot(X[y], W[c], preferred_element_type=jnp.float32)
+
+    def hand_over(c):
+        got(R.at[c], s_recv.at[c])
+        S2[c] = (Q[c] + R[c].astype(jnp.float32)).astype(S2.dtype)
+        push(S2.at[c], R2.at[c], z_send.at[c], z_recv.at[c], (g, along, b))
+
+    def h_piece(c, k):
+        return H.at[y, c, :, lanes(k)]
+
+    def finish(c):
+        got(R.at[c], s_recv.at[c])
+        got(R2.at[c], z_recv.at[c])
+        both = Q[c] + R[c].astype(jnp.float32) + R2[c].astype(jnp.float32)
+        hidden = (jax.nn.silu(both[:, :LANES]) * both[:, LANES:]).astype(hs.dtype)
+        hs[c] = hidden
+        push(hs.at[c], h_piece(c, b), h_send.at[c, 0], h_recv.at[c, b], (g, facing, a))
+        push(hs.at[c], h_piece(c, b), h_send.at[c, 1], h_recv.at[c, b], (g, along, a))
+
+        @pl.when(own)
+        def _():
+            H[y, c, :, lanes(b)] = hidden
+
+        @pl.when(foreign)
+        def _():
+            push(hs.at[c], h_piece(c, b), h_send.at[c, 2], h_recv.at[c, b], other)
+
+    def spread(c):
+        block = H.at[y, c]
+
+        @pl.when(jnp.logical_and(own, inner))
+        def _():
+            got(h_piece(c, 1 - b), h_recv.at[c, 1 - b])
+
+        @pl.when(jnp.logical_and(own, outer))
+        def _():
+            for k in range(B):
+                got(h_piece(c, k), h_recv.at[c, k])
+
+        @pl.when(jnp.logical_and(foreign, inner))
+        def _():
+            for k in range(B):
+                got(h_piece(c, k), h_recv.at[c, k])
+            push(block, block, r_send.at[c], r_recv.at[c], (g, along, b))
+
+        @pl.when(jnp.logical_and(foreign, outer))
+        def _():
+            got(block, r_recv.at[c])
+
+        push(block, block, y_send.at[c], y_recv.at[c], beside)
+
+    def project(c):
+        got(H.at[1 - y, c], y_recv.at[c])
+        for k in range(2):
+            acc[k] += jnp.dot(H[k, c], D[c], preferred_element_type=jnp.float32)
+
+    def step(c, role, stage):
+        @pl.when(jnp.logical_and(role, jnp.logical_and(c >= 0, c < chunks)))
+        def _():
+            stage(c)
+
+    weights_arrive(0)
+    for load in loads:
+        load.wait()
+    for d in (1, 2, 3):
+        block = x_block(partner(d), b)
+        got(block, t_recv.at[d])
+        push(block, block, c_send.at[d], c_recv.at[d], other)
+    for d in (1, 2, 3):
+        got(x_block(partner(d), 1 - b), c_recv.at[d])
+    for c in range(chunks):
+        down_loads[c].wait()
+        got(d_block(c, 1 - b), d_recv.at[c])
+
+    always = n > 0
+
+    def body(i, carry):
+        step(i - 3, inner, finish)
+        step(i - 2, outer, hand_over)
+        step(i - 1, always, partial_sums)
+        step(i - 4, own, spread)
+        step(i - 5, own, project)
+        late = 2 * (i - chunks)
+        for k in range(2):
+            step(late + k, foreign, spread)
+        for k in range(2):
+            step(late - 2 + k, foreign, project)
+        step(i, always, weights_arrive)
+        return carry
+
+    lax.fori_loop(1, chunks + 5, body, 0)
+
+    for i in range(h):
+        out[pl.ds(i * rows, rows), :] = acc[i % 2, pl.ds(i // 2 * rows, rows), :].astype(out.dtype)
+
+    for d in (1, 2, 3):
+        sent(x_block(j, 0), t_send.at[d])
+        sent(x_block(j, 0), c_send.at[d])
+
+    def drain(c, carry):
+        for k in range(2):
+            sent(w_piece(c, k), w_send.at[c, k])
+        for e in range(1, G):
+            sent(W.at[c, landed, :], x_send.at[e, c])
+        sent(d_block(c, b), d_send.at[c])
+        sent(S.at[c], s_send.at[c])
+        sent(H.at[y, c], y_send.at[c])
+
+        @pl.when(outer)
+        def _():
+            sent(S2.at[c], z_send.at[c])
+
+        @pl.when(inner)
+        def _():
+            sent(hs.at[c], h_send.at[c, 0])
+            sent(hs.at[c], h_send.at[c, 1])
+
+        @pl.when(jnp.logical_and(inner, foreign))
+        def _():
+            sent(hs.at[c], h_send.at[c, 2])
+            sent(H.at[y, c], r_send.at[c])
+
+        return carry
+
+    lax.fori_loop(0, chunks, drain, 0)
+
+
+def column_local(G, n, B, tokens, gate_weight, up_weight, down_weight):
+    h = n // B
+    rows = tokens.shape[0]
+    depth, wide = gate_weight.shape
+    columns = down_weight.shape[1]
+    chunks = wide // LANES
+    half = h // 2 * rows
+    dtype = tokens.dtype
+    DMA = pltpu.SemaphoreType.DMA
+    pair = pltpu.VMEM((chunks, half, 2 * LANES), dtype)
+    return pl.pallas_call(
+        functools.partial(column_layer, G, n, B),
+        out_shape=jax.ShapeDtypeStruct((h * rows, columns), dtype),
+        in_specs=[ANY] * 4,
+        out_specs=pl.BlockSpec(memory_space=pltpu.VMEM),
+        scratch_shapes=[
+            pltpu.VMEM((2, half, 2 * depth), dtype),
+            pltpu.VMEM((chunks, 2 * depth, 2 * LANES), dtype),
+            pltpu.VMEM((chunks, B * LANES, columns), dtype),
+            pltpu.VMEM((chunks, half, 2 * LANES), jnp.float32),
+            pair, pair, pair, pair,
+            pltpu.VMEM((chunks, half, LANES), dtype),
+            pltpu.VMEM((2, chunks, half, B * LANES), dtype),
+            pltpu.VMEM((2, half, columns), jnp.float32),
+            DMA((chunks, 2)), DMA((2,)), DMA((chunks,)),
+            DMA((chunks, 2)), DMA((chunks, 2)),
+            DMA((G, chunks)), DMA((G, chunks)),
+            DMA((4,)), DMA((4,)), DMA((4,)), DMA((4,)),
+            DMA((chunks,)), DMA((chunks,)),
+            DMA((chunks,)), DMA((chunks,)),
+            DMA((chunks,)), DMA((chunks,)),
+            DMA((chunks, 3)), DMA((chunks, B)),
+            DMA((chunks,)), DMA((chunks,)),
+            DMA((chunks,)), DMA((chunks,)),
+        ],
+        compiler_params=pltpu.CompilerParams(
+            collective_id=0, has_side_effects=True, vmem_limit_bytes=63_000_000
+        ),
+        name="layer",
+    )(tokens, gate_weight, up_weight, down_weight)
+
+
 def solution(mesh):
     shape = dict(mesh.shape)
+    sizes = shape["groups"], shape["tp"], shape["blk"]
+    kernel = column_local if sizes[1:] == (8, 2) else local
     return jax.shard_map(
-        functools.partial(local, shape["groups"], shape["tp"], shape["blk"]),
+        functools.partial(kernel, *sizes),
         mesh=mesh,
         in_specs=(P(("groups", "tp"), None), P("tp", "blk"), P("tp", "blk"), P("blk", "tp")),
         out_specs=P(("groups", "blk"), "tp"),

time: 186 us -> 166 us (0.89)
  the two profiles are of different devices: /device:TPU:1 before, /device:TPU:26 now
where the time goes in v1:
time: 166 us
  Pallas kernels  163 us (98%)
  local copies, waits for them, and re-layouts  2.87 us (2%)
    pallas_call x1, Pallas kernels, column_local(): pl.pallas_call(functools.partial(column_layer, G, n, B), out_shape=jax.Sh...  163 us

profile of v1, /device:TPU:26, one launch (start us, length us, event | category | flops | bytes accessed | tf_op | source)
XLA Modules:
  0.0 166.2 jit_solution(10171339118465620042)
XLA Ops:
  0.0 163.3 %layer.1 = bf16[1024,896]{1,0:T(8,128)(2,1)} custom-call(bf16[256,7168]{1,0:T(8,128)(2,1)} %tok.1, bf16[896,1024]{1,0:T(8,128)(2,1)} %gate.1, bf16[896,1024]{1,0:T(8,128)(2,1)} %up.1, bf16[1024,896]{1,0:T(8,128)(2,1)} %down.1), custom_call_target="tpu_custom_call" | custom-call | tf_op jit(solution)/shard_map/layer/pallas_call | solution.py:531
  163.3 2.9 %copy.6 = bf16[1024,896]{1,0:T(8,128)(2,1)} copy(bf16[1024,896]{1,0:T(8,128)(2,1)} %layer.1) | data formatting | bytes 3670016

commit v2 on v0

--- a/solution.py
+++ b/solution.py
@@ -270,10 +270,475 @@
     )(tokens, gate_weight, up_weight, down_weight)
 
 
+LANES = 128
+
+
+def column_layer(
+    G, n, B,
+    tok, gate, up, down, out,
+    X, W, D, Q, S, R, hs, H, acc,
+    l_w, l_x, l_d,
+    p_send, p_recv, q_send, q_recv, f_send, f_recv, x_send, x_recv,
+    t_send, t_recv, c_send, c_recv, d_send, d_recv,
+    z_send, z_recv, h_send, h_recv, r_send, r_recv, y_send, y_recv,
+):
+    g, t, b = lax.axis_index("groups"), lax.axis_index("tp"), lax.axis_index("blk")
+    h = n // B
+    z, y, j, a = t // 2, t % 2, t % h, t // h
+    last = n // 2 - 1
+    mz = last - z
+    inner = z % 2 + a == 1
+    outer = z % 2 + a != 1
+    own, foreign = b == a, b != a
+    rows, depth, wide = tok.shape[0], gate.shape[0], gate.shape[1]
+    part, run, half = depth // G, 2 * depth, h // 2 * rows
+    chunks = wide // LANES // 2
+    other = (g, t, 1 - b)
+    beside = (g, flip1(t), b)
+    along = flip2(t)
+    facing = 2 * mz + y
+
+    greet(
+        [(g, chip, c) for chip in (along, facing) for c in range(B)]
+        + [other, beside]
+        + [((g + e) % G, t, b) for e in range(1, G)]
+    )
+
+    def remote(src, dst, send, recv, device):
+        return pltpu.make_async_remote_copy(
+            src_ref=src, dst_ref=dst, send_sem=send, recv_sem=recv,
+            device_id=device, device_id_type=MESH,
+        )
+
+    def push(*copy):
+        remote(*copy).start()
+
+    def got(ref, sem):
+        remote(ref, ref, sem, sem, other).wait_recv()
+
+    def sent(ref, sem):
+        remote(ref, ref, sem, sem, other).wait_send()
+
+    def lanes(k):
+        return pl.ds(pl.multiple_of(k * LANES, LANES), LANES)
+
+    share = pl.ds(pl.multiple_of(g * part, 16), part)
+
+    def landing(k, e):
+        return pl.ds(pl.multiple_of(k * depth + e * part, 16), part)
+
+    def w_piece(c, slot, k):
+        return W.at[c, landing(slot, g), pl.ds(k * LANES, LANES)]
+
+    def w_share(c, slot, e):
+        return W.at[c, landing(slot, e), :]
+
+    def depth_of(row):
+        return pl.ds(pl.multiple_of(row * run, LANES), run)
+
+    def x_block(i, k):
+        return X.at[
+            i // 2, pl.ds(pl.multiple_of(i % 2 * rows, 16), rows),
+            pl.ds(pl.multiple_of(k * run, LANES), run),
+        ]
+
+    def d_block(i, k):
+        return D.at[i, pl.ds(pl.multiple_of(k * LANES, LANES), LANES), :]
+
+    near, beyond, diagonal = flip1(j), flip2(j), flip1(flip2(j))
+    z2 = along // 2
+    row_there = z2 + b * (last - 2 * z2)
+    row_here = z + b * (mz - z)
+
+    def send_across(c):
+        for k in range(2):
+            push(
+                (gate, up)[k].at[share, lanes(y * chunks + c)], w_piece(c, 2 + y, k),
+                p_send.at[c, k], p_recv.at[c, k], (g, facing, b),
+            )
+
+    def send_beside(c):
+        for k in range(2):
+            push(
+                (gate, up)[k].at[share, lanes((1 - y) * chunks + c)], w_piece(c, y, k),
+                q_send.at[c, k], q_recv.at[c, k], beside,
+            )
+
+    push(tok.at[:, depth_of(row_there)], x_block(j, b), t_send.at[0], t_recv.at[0], (g, along, b))
+    send_beside(0)
+    push(tok.at[:, depth_of(row_here)], x_block(j, b), t_send.at[1], t_recv.at[1], beside)
+    send_beside(1)
+
+    @pl.when(inner)
+    def _():
+        send_across(0)
+        send_across(1)
+
+    loads = []
+    for k, row in enumerate((z, mz)):
+        loads.append(pltpu.make_async_copy(tok.at[:, depth_of(row)], x_block(j, k), l_x.at[k]))
+    for c in range(chunks):
+        for k in range(2):
+            loads.append(pltpu.make_async_copy(
+                (gate, up)[k].at[:, lanes(y * chunks + c)],
+                W.at[c, pl.ds(pl.multiple_of(y * depth, LANES), depth), pl.ds(k * LANES, LANES)],
+                l_w.at[c, k],
+            ))
+    for i in range(2 * chunks):
+        piece = down.at[pl.ds(i * LANES, LANES), :]
+        loads.append(pltpu.make_async_copy(piece, d_block(i, b), l_d.at[i]))
+        push(piece, d_block(i, b), d_send.at[i], d_recv.at[i], other)
+    for load in loads:
+        load.start()
+    acc[...] = jnp.zeros_like(acc)
+
+    def swap(c, slot, i):
+        block = w_share(c, slot, g)
+        for e in range(1, G):
+            push(block, block, x_send.at[e, c, i], x_recv.at[e, c, i], ((g + e) % G, t, b))
+
+    def from_beside(c):
+        for k in range(2):
+            got(w_piece(c, 1 - y, k), q_recv.at[c, k])
+        swap(c, 1 - y, 0)
+
+    def relay(c):
+        push(w_share(c, 1 - y, g), w_share(c, 3 - y, g), f_send.at[c], f_recv.at[c], (g, facing, b))
+
+    def from_facing(c):
+        for k in range(2):
+            got(w_piece(c, 2 + y, k), p_recv.at[c, k])
+        swap(c, 2 + y, 1)
+
+    def relayed(c):
+        got(w_share(c, 3 - y, g), f_recv.at[c])
+        swap(c, 3 - y, 2)
+
+    def pass_tokens(i, k):
+        block = x_block(i, b)
+        got(block, t_recv.at[k])
+        push(block, block, c_send.at[k], c_recv.at[k], other)
+
+    def ready(c):
+        for e in range(1, G):
+            for i, slot in enumerate((1 - y, 2 + y, 3 - y)):
+                got(w_share(c, slot, (g + G - e) % G), x_recv.at[e, c, i])
+
+    def multiply(c, r):
+        return jnp.dot(X[r], W[c], preferred_element_type=jnp.float32)
+
+    def keep(c, r):
+        Q[c, r] = multiply(c, r)
+
+    def give(c, r):
+        S[c, r] = multiply(c, r).astype(S.dtype)
+        push(S.at[c, r], R.at[c, r], z_send.at[c, r], z_recv.at[c, r], (g, along, b))
+
+    def h_piece(c, r, k):
+        return H.at[y, c, r, :, lanes(k)]
+
+    def finish(c, r):
+        got(R.at[c, r], z_recv.at[c, r])
+        both = Q[c, r] + R[c, r].astype(jnp.float32)
+        hidden = (jax.nn.silu(both[:, :LANES]) * both[:, LANES:]).astype(hs.dtype)
+        hs[c, r] = hidden
+        block, there = hs.at[c, r], h_piece(c, r, b)
+        push(block, there, h_send.at[c, r, 0], h_recv.at[c, r, b], (g, facing, a))
+        push(block, there, h_send.at[c, r, 1], h_recv.at[c, r, b], (g, along, a))
+
+        @pl.when(own)
+        def _():
+            H[y, c, r, :, lanes(b)] = hidden
+
+        @pl.when(foreign)
+        def _():
+            push(block, there, h_send.at[c, r, 2], h_recv.at[c, r, b], other)
+
+    def onward(c, r):
+        push(H.at[y, c, r], H.at[y, c, r], y_send.at[c, r], y_recv.at[c, r], beside)
+
+    def spread_own_inner(c, r):
+        got(h_piece(c, r, 1 - b), h_recv.at[c, r, 1 - b])
+        onward(c, r)
+
+    def spread_own_outer(c, r):
+        for k in range(B):
+            got(h_piece(c, r, k), h_recv.at[c, r, k])
+        onward(c, r)
+
+    def spread_foreign_inner(c, r):
+        for k in range(B):
+            got(h_piece(c, r, k), h_recv.at[c, r, k])
+        block = H.at[y, c, r]
+        push(block, block, r_send.at[c, r], r_recv.at[c, r], (g, along, b))
+        onward(c, r)
+
+    def spread_foreign_outer(c, r):
+        got(H.at[y, c, r], r_recv.at[c, r])
+        onward(c, r)
+
+    def project(c, r):
+        got(H.at[1 - y, c, r], y_recv.at[c, r])
+        acc[r] += jnp.dot(H[0, c, r], D[c], preferred_element_type=jnp.float32) + jnp.dot(
+            H[1, c, r], D[chunks + c], preferred_element_type=jnp.float32
+        )
+
+    rz = z % 2
+
+    def pass_beyond():
+        block = x_block(beyond, b)
+        got(block, t_recv.at[0])
+        push(block, block, t_send.at[2], t_recv.at[2], beside)
+        push(block, block, c_send.at[0], c_recv.at[0], other)
+        for c in range(2, chunks):
+            send_beside(c)
+
+    def held(i, k):
+        got(x_block(i, 1 - b), c_recv.at[k])
+
+    def settle():
+        for load in loads:
+            load.wait()
+
+    def settle_down():
+        for i in range(2 * chunks):
+            got(d_block(i, 1 - b), d_recv.at[i])
+
+    def when(role, stage, *args):
+        @pl.when(role)
+        def _():
+            stage(*args)
+
+    halves = (rz, 1 - rz)
+    end = chunks - 1
+
+    def tokens_complete():
+        pass_tokens(diagonal, 2)
+        held(beyond, 0)
+        held(diagonal, 2)
+
+    def each(stage, c, order):
+        for r in order:
+            stage(c, r)
+
+    @pl.when(inner)
+    def _():
+        first = (1 - rz, rz)
+        from_beside(0)
+        relay(0)
+        send_across(2)
+        from_facing(0)
+        from_facing(1)
+        relayed(0)
+        pass_beyond()
+        pass_tokens(near, 1)
+        settle()
+        held(near, 1)
+        ready(0)
+        keep(0, rz)
+        from_beside(1)
+        relay(1)
+        tokens_complete()
+        keep(0, 1 - rz)
+        finish(0, 1 - rz)
+        from_beside(2)
+        relay(2)
+        send_across(3)
+        when(own, spread_own_inner, 0, 1 - rz)
+        finish(0, rz)
+        from_beside(3)
+        relay(3)
+        when(own, spread_own_inner, 0, rz)
+        settle_down()
+        relayed(1)
+        from_facing(2)
+        when(own, project, 0, 1 - rz)
+        ready(1)
+        each(keep, 1, first)
+        relayed(2)
+        each(finish, 1, first)
+        when(own, each, spread_own_inner, 1, first)
+        from_facing(3)
+        when(foreign, each, spread_foreign_inner, 0, halves)
+        ready(2)
+        each(keep, 2, first)
+        relayed(3)
+        each(finish, 2, first)
+        when(own, each, spread_own_inner, 2, first)
+        when(own, project, 0, rz)
+        when(foreign, each, spread_foreign_inner, 1, halves)
+        ready(3)
+        each(keep, 3, first)
+
+        @pl.when(own)
+        def _():
+            each(project, 1, first)
+            for r in first:
+                finish(3, r)
+                spread_own_inner(3, r)
+            for c in (2, 3):
+                each(project, c, first)
+
+        @pl.when(foreign)
+        def _():
+            each(project, 0, halves)
+            spread_foreign_inner(2, rz)
+            finish(3, 1 - rz)
+            spread_foreign_inner(2, 1 - rz)
+            finish(3, rz)
+            each(project, 1, halves)
+            each(spread_foreign_inner, 3, halves)
+            each(project, 2, halves)
+            each(project, 3, halves)
+
+    @pl.when(outer)
+    def _():
+        far = (1 - rz, rz)
+        from_beside(0)
+        sent(x_block(j, 0), t_send.at[0])
+        send_across(0)
+        relay(0)
+        send_across(1)
+        pass_beyond()
+        pass_tokens(near, 1)
+        from_facing(0)
+        from_beside(1)
+        relay(1)
+        for c in range(2, chunks):
+            send_across(c)
+        relayed(0)
+        from_facing(1)
+        settle()
+        held(near, 1)
+        ready(0)
+        give(0, rz)
+        relayed(1)
+        tokens_complete()
+        give(0, 1 - rz)
+        from_facing(2)
+        from_beside(2)
+        relay(2)
+        ready(1)
+        give(1, rz)
+        from_beside(3)
+        relay(3)
+        give(1, 1 - rz)
+        from_facing(3)
+        settle_down()
+        relayed(2)
+        when(own, spread_own_outer, 0, rz)
+        relayed(3)
+        ready(2)
+        each(give, 2, halves)
+        ready(3)
+        each(give, 3, halves)
+        when(own, spread_own_outer, 0, 1 - rz)
+
+        @pl.when(own)
+        def _():
+            for c in (1, 2, 3):
+                each(spread_own_outer, c, halves)
+                each(project, c - 1, halves)
+            each(project, 3, halves)
+
+        @pl.when(foreign)
+        def _():
+            each(spread_foreign_outer, 0, far)
+            for c in (1, 2, 3):
+                each(spread_foreign_outer, c, far)
+                each(project, c - 1, far)
+            each(project, 3, far)
+
+    for r in range(2):
+        out[pl.ds(r * half, half), :] = acc[r].astype(out.dtype)
+
+    when(inner, sent, x_block(j, 0), t_send.at[0])
+    for k in range(3):
+        if k:
+            sent(x_block(j, 0), t_send.at[k])
+        sent(x_block(j, 0), c_send.at[k])
+    for i in range(2 * chunks):
+        sent(d_block(i, b), d_send.at[i])
+
+    def drain(c, carry):
+        for k in range(2):
+            sent(w_piece(c, 0, k), p_send.at[c, k])
+            sent(w_piece(c, 0, k), q_send.at[c, k])
+        sent(w_share(c, 0, g), f_send.at[c])
+        for e in range(1, G):
+            for i in range(3):
+                sent(w_share(c, 0, g), x_send.at[e, c, i])
+        for r in range(2):
+            sent(H.at[y, c, r], y_send.at[c, r])
+
+            @pl.when(outer)
+            def _():
+                sent(S.at[c, r], z_send.at[c, r])
+
+            @pl.when(inner)
+            def _():
+                sent(hs.at[c, r], h_send.at[c, r, 0])
+                sent(hs.at[c, r], h_send.at[c, r, 1])
+
+            @pl.when(jnp.logical_and(inner, foreign))
+            def _():
+                sent(hs.at[c, r], h_send.at[c, r, 2])
+                sent(H.at[y, c, r], r_send.at[c, r])
+
+        return carry
+
+    lax.fori_loop(0, chunks, drain, 0)
+
+
+def column_local(G, n, B, tokens, gate_weight, up_weight, down_weight):
+    h = n // B
+    rows = tokens.shape[0]
+    depth, wide = gate_weight.shape
+    columns = down_weight.shape[1]
+    chunks = wide // LANES // 2
+    half = h // 2 * rows
+    dtype = tokens.dtype
+    DMA = pltpu.SemaphoreType.DMA
+    pair = pltpu.VMEM((chunks, 2, half, 2 * LANES), dtype)
+    return pl.pallas_call(
+        functools.partial(column_layer, G, n, B),
+        out_shape=jax.ShapeDtypeStruct((h * rows, columns), dtype),
+        in_specs=[ANY] * 4,
+        out_specs=pl.BlockSpec(memory_space=pltpu.VMEM),
+        scratch_shapes=[
+            pltpu.VMEM((2, half, 4 * depth), dtype),
+            pltpu.VMEM((chunks, 4 * depth, 2 * LANES), dtype),
+            pltpu.VMEM((2 * chunks, B * LANES, columns), dtype),
+            pltpu.VMEM((chunks, 2, half, 2 * LANES), jnp.float32),
+            pair, pair,
+            pltpu.VMEM((chunks, 2, half, LANES), dtype),
+            pltpu.VMEM((2, chunks, 2, half, B * LANES), dtype),
+            pltpu.VMEM((2, half, columns), jnp.float32),
+            DMA((chunks, 2)), DMA((2,)), DMA((2 * chunks,)),
+            DMA((chunks, 2)), DMA((chunks, 2)),
+            DMA((chunks, 2)), DMA((chunks, 2)),
+            DMA((chunks,)), DMA((chunks,)),
+            DMA((G, chunks, 3)), DMA((G, chunks, 3)),
+            DMA((3,)), DMA((3,)), DMA((3,)), DMA((3,)),
+            DMA((2 * chunks,)), DMA((2 * chunks,)),
+            DMA((chunks, 2)), DMA((chunks, 2)),
+            DMA((chunks, 2, 3)), DMA((chunks, 2, B)),
+            DMA((chunks, 2)), DMA((chunks, 2)),
+            DMA((chunks, 2)), DMA((chunks, 2)),
+        ],
+        compiler_params=pltpu.CompilerParams(
+            collective_id=0, has_side_effects=True, vmem_limit_bytes=63_000_000
+        ),
+        name="layer",
+    )(tokens, gate_weight, up_weight, down_weight)
+
+
 def solution(mesh):
     shape = dict(mesh.shape)
+    sizes = shape["groups"], shape["tp"], shape["blk"]
+    kernel = column_local if sizes[1:] == (8, 2) else local
     return jax.shard_map(
-        functools.partial(local, shape["groups"], shape["tp"], shape["blk"]),
+        functools.partial(kernel, *sizes),
         mesh=mesh,
         in_specs=(P(("groups", "tp"), None), P("tp", "blk"), P("tp", "blk"), P("blk", "tp")),
         out_specs=P(("groups", "blk"), "tp"),

time: 186 us -> 147 us (0.79)
  Pallas kernels: 182 us -> 144 us
    pallas_call x1, Pallas kernels: 182 us -> 144 us  [column_local(): pl.pallas_call(functools.partial(column_layer, G, n, B), out_shape=jax.Sh...]
where the time goes in v2:
time: 147 us
  Pallas kernels  144 us (98%)
  local copies, waits for them, and re-layouts  2.87 us (2%)
    pallas_call x1, Pallas kernels, column_local(): pl.pallas_call(functools.partial(column_layer, G, n, B), out_shape=jax.Sh...  144 us

profile of v2, /device:TPU:1, one launch (start us, length us, event | category | flops | bytes accessed | tf_op | source)
XLA Modules:
  0.0 147.2 jit_solution(15342892736711148101)
XLA Ops:
  0.0 144.3 %layer.1 = bf16[1024,896]{1,0:T(8,128)(2,1)} custom-call(bf16[256,7168]{1,0:T(8,128)(2,1)} %tok.1, bf16[896,1024]{1,0:T(8,128)(2,1)} %gate.1, bf16[896,1024]{1,0:T(8,128)(2,1)} %up.1, bf16[1024,896]{1,0:T(8,128)(2,1)} %down.1), custom_call_target="tpu_custom_call" | custom-call | tf_op jit(solution)/shard_map/layer/pallas_call | solution.py:703
  144.3 2.9 %copy.6 = bf16[1024,896]{1,0:T(8,128)(2,1)} copy(bf16[1024,896]{1,0:T(8,128)(2,1)} %layer.1) | data formatting | bytes 3670016

commit v3 on v2

--- a/solution.py
+++ b/solution.py
@@ -280,7 +280,7 @@
     l_w, l_x, l_d,
     p_send, p_recv, q_send, q_recv, f_send, f_recv, x_send, x_recv,
     t_send, t_recv, c_send, c_recv, d_send, d_recv,
-    z_send, z_recv, h_send, h_recv, r_send, r_recv, y_send, y_recv,
+    z_send, z_recv, h_send, h_recv, r_send, r_recv, y_send, y_recv, word,
 ):
     g, t, b = lax.axis_index("groups"), lax.axis_index("tp"), lax.axis_index("blk")
     h = n // B
@@ -298,11 +298,23 @@
     along = flip2(t)
     facing = 2 * mz + y
 
-    greet(
-        [(g, chip, c) for chip in (along, facing) for c in range(B)]
-        + [other, beside]
-        + [((g + e) % G, t, b) for e in range(1, G)]
-    )
+    near_by = [(g, along, c) for c in range(B)] + [other, beside]
+    near_by += [((g + e) % G, t, b) for e in range(1, G)]
+    opposite = [(g, facing, c) for c in range(B)]
+
+    @pl.when(inner)
+    def _():
+        greet(near_by + opposite)
+
+    @pl.when(outer)
+    def _():
+        greet(near_by)
+
+    def tell(device):
+        pl.semaphore_signal(word, inc=1, device_id=device, device_id_type=MESH)
+
+    def hear():
+        pl.semaphore_wait(word, 1)
 
     def remote(src, dst, send, recv, device):
         return pltpu.make_async_remote_copy(
@@ -366,13 +378,17 @@
 
     push(tok.at[:, depth_of(row_there)], x_block(j, b), t_send.at[0], t_recv.at[0], (g, along, b))
     send_beside(0)
+    send_beside(1)
     push(tok.at[:, depth_of(row_here)], x_block(j, b), t_send.at[1], t_recv.at[1], beside)
-    send_beside(1)
+    send_beside(2)
 
     @pl.when(inner)
     def _():
         send_across(0)
         send_across(1)
+        tell((g, facing, b))
+        hear()
+        tell((g, along, b))
 
     loads = []
     for k, row in enumerate((z, mz)):
@@ -400,6 +416,8 @@
     def from_beside(c):
         for k in range(2):
             got(w_piece(c, 1 - y, k), q_recv.at[c, k])
+
+    def swap_beside(c):
         swap(c, 1 - y, 0)
 
     def relay(c):
@@ -490,7 +508,7 @@
         got(block, t_recv.at[0])
         push(block, block, t_send.at[2], t_recv.at[2], beside)
         push(block, block, c_send.at[0], c_recv.at[0], other)
-        for c in range(2, chunks):
+        for c in range(3, chunks):
             send_beside(c)
 
     def held(i, k):
@@ -526,9 +544,13 @@
         first = (1 - rz, rz)
         from_beside(0)
         relay(0)
+        swap_beside(0)
         send_across(2)
         from_facing(0)
         from_facing(1)
+        from_beside(1)
+        relay(1)
+        swap_beside(1)
         relayed(0)
         pass_beyond()
         pass_tokens(near, 1)
@@ -536,114 +558,134 @@
         held(near, 1)
         ready(0)
         keep(0, rz)
-        from_beside(1)
-        relay(1)
+        from_beside(2)
+        relay(2)
         tokens_complete()
+        from_facing(2)
         keep(0, 1 - rz)
         finish(0, 1 - rz)
-        from_beside(2)
-        relay(2)
         send_across(3)
         when(own, spread_own_inner, 0, 1 - rz)
+        relayed(1)
+        from_beside(3)
+        swap_beside(2)
         finish(0, rz)
-        from_beside(3)
-        relay(3)
         when(own, spread_own_inner, 0, rz)
         settle_down()
-        relayed(1)
-        from_facing(2)
-        when(own, project, 0, 1 - rz)
         ready(1)
-        each(keep, 1, first)
+        keep(1, 1 - rz)
         relayed(2)
-        each(finish, 1, first)
-        when(own, each, spread_own_inner, 1, first)
+        when(foreign, spread_foreign_inner, 0, rz)
+        finish(1, 1 - rz)
+        relay(3)
+        when(own, spread_own_inner, 1, 1 - rz)
+        keep(1, rz)
         from_facing(3)
-        when(foreign, each, spread_foreign_inner, 0, halves)
+        swap_beside(3)
         ready(2)
-        each(keep, 2, first)
+        keep(2, 1 - rz)
+        when(foreign, spread_foreign_inner, 0, 1 - rz)
+        finish(1, rz)
+        when(own, spread_own_inner, 1, rz)
+        keep(2, rz)
+        when(foreign, spread_foreign_inner, 1, rz)
+        finish(2, 1 - rz)
         relayed(3)
-        each(finish, 2, first)
-        when(own, each, spread_own_inner, 2, first)
-        when(own, project, 0, rz)
-        when(foreign, each, spread_foreign_inner, 1, halves)
+        when(own, spread_own_inner, 2, 1 - rz)
+        when(own, each, project, 0, first)
+        finish(2, rz)
+        when(own, spread_own_inner, 2, rz)
+        when(foreign, spread_foreign_inner, 1, 1 - rz)
+        when(foreign, spread_foreign_inner, 2, rz)
         ready(3)
-        each(keep, 3, first)
+        keep(3, 1 - rz)
+        when(foreign, spread_foreign_inner, 2, 1 - rz)
+        keep(3, rz)
 
         @pl.when(own)
         def _():
-            each(project, 1, first)
-            for r in first:
-                finish(3, r)
-                spread_own_inner(3, r)
+            finish(3, 1 - rz)
+            project(1, 1 - rz)
+            spread_own_inner(3, 1 - rz)
+            finish(3, rz)
+            project(1, rz)
+            spread_own_inner(3, rz)
             for c in (2, 3):
                 each(project, c, first)
 
         @pl.when(foreign)
         def _():
-            each(project, 0, halves)
-            spread_foreign_inner(2, rz)
-            finish(3, 1 - rz)
-            spread_foreign_inner(2, 1 - rz)
-            finish(3, rz)
-            each(project, 1, halves)
-            each(spread_foreign_inner, 3, halves)
-            each(project, 2, halves)
+            each(finish, 3, first)
+            spread_foreign_inner(3, rz)
+            project(0, rz)
+            spread_foreign_inner(3, 1 - rz)
+            project(0, 1 - rz)
+            for c in (1, 2):
+                each(project, c, halves)
             each(project, 3, halves)
 
     @pl.when(outer)
     def _():
         far = (1 - rz, rz)
         from_beside(0)
+        swap_beside(0)
+        hear()
         sent(x_block(j, 0), t_send.at[0])
         send_across(0)
         relay(0)
         send_across(1)
         pass_beyond()
-        pass_tokens(near, 1)
-        from_facing(0)
         from_beside(1)
         relay(1)
-        for c in range(2, chunks):
-            send_across(c)
+        send_across(2)
+        from_facing(0)
+        pass_tokens(near, 1)
         relayed(0)
+        swap_beside(1)
+        from_beside(2)
+        relay(2)
+        send_across(3)
         from_facing(1)
         settle()
         held(near, 1)
         ready(0)
         give(0, rz)
         relayed(1)
+        from_facing(2)
         tokens_complete()
         give(0, 1 - rz)
-        from_facing(2)
-        from_beside(2)
-        relay(2)
+        swap_beside(2)
         ready(1)
         give(1, rz)
         from_beside(3)
         relay(3)
+        relayed(2)
         give(1, 1 - rz)
         from_facing(3)
+        swap_beside(3)
         settle_down()
-        relayed(2)
         when(own, spread_own_outer, 0, rz)
-        relayed(3)
         ready(2)
         each(give, 2, halves)
+        relayed(3)
+        when(own, spread_own_outer, 0, 1 - rz)
+        when(own, spread_own_outer, 1, rz)
+        when(foreign, spread_foreign_outer, 0, 1 - rz)
         ready(3)
         each(give, 3, halves)
-        when(own, spread_own_outer, 0, 1 - rz)
 
         @pl.when(own)
         def _():
-            for c in (1, 2, 3):
+            spread_own_outer(1, 1 - rz)
+            each(project, 0, halves)
+            for c in (2, 3):
                 each(spread_own_outer, c, halves)
                 each(project, c - 1, halves)
             each(project, 3, halves)
 
         @pl.when(foreign)
         def _():
-            each(spread_foreign_outer, 0, far)
+            spread_foreign_outer(0, rz)
             for c in (1, 2, 3):
                 each(spread_foreign_outer, c, far)
                 each(project, c - 1, far)
@@ -725,6 +767,7 @@
             DMA((chunks, 2, 3)), DMA((chunks, 2, B)),
             DMA((chunks, 2)), DMA((chunks, 2)),
             DMA((chunks, 2)), DMA((chunks, 2)),
+            pltpu.SemaphoreType.REGULAR,
         ],
         compiler_params=pltpu.CompilerParams(
             collective_id=0, has_side_effects=True, vmem_limit_bytes=63_000_000

time: 147 us -> 138 us (0.939)
  Pallas kernels: 144 us -> 135 us
    pallas_call x1, Pallas kernels: 144 us -> 135 us  [column_local(): pl.pallas_call(functools.partial(column_layer, G, n, B), out_shape=jax.Sh...]
where the time goes in v3:
time: 138 us
  Pallas kernels  135 us (98%)
  local copies, waits for them, and re-layouts  2.87 us (2%)
    pallas_call x1, Pallas kernels, column_local(): pl.pallas_call(functools.partial(column_layer, G, n, B), out_shape=jax.Sh...  135 us
    unnamed x1, local copies, waits for them, and re-layouts  2.87 us

profile of v3, /device:TPU:1, one launch (start us, length us, event | category | flops | bytes accessed | tf_op | source)
XLA Modules:
  0.0 137.8 jit_solution(10339437406352034858)
XLA Ops:
  0.0 134.9 %layer.1 = bf16[1024,896]{1,0:T(8,128)(2,1)} custom-call(bf16[256,7168]{1,0:T(8,128)(2,1)} %tok.1, bf16[896,1024]{1,0:T(8,128)(2,1)} %gate.1, bf16[896,1024]{1,0:T(8,128)(2,1)} %up.1, bf16[1024,896]{1,0:T(8,128)(2,1)} %down.1), custom_call_target="tpu_custom_call" | custom-call | tf_op jit(solution)/shard_map/layer/pallas_call | solution.py:745
  134.9 2.9 %copy.6 = bf16[1024,896]{1,0:T(8,128)(2,1)} copy(bf16[1024,896]{1,0:T(8,128)(2,1)} %layer.1) | data formatting | bytes 3670016
